TPU v7x, 256 devices: a whole 4x4x8 slice. The times are simulated.
256 devices in a mesh: blk: 128 (over y, z, x), rep: 2 (over core).
Axes of the slice: x: 4, y: 4, z: 8, core: 2. Of those that a mesh axis runs over, the one named last changes fastest.
Arguments:
- x_points: bfloat16 [131072, 512], P('blk'), may hold values from -8 to 8
- y_points: bfloat16 [131072, 512], P('blk'), may hold values from -8 to 8
- first_masses: float32 [131072], P('blk'), may hold values from 0.25 to 4
- second_masses: float32 [131072], P('blk'), may hold values from 0.25 to 4
- f_start: float32 [131072], P('blk'), may hold values from 0.55 to 20
- g_start: float32 [131072], P('blk'), may hold values from 0.55 to 20
- block_owner: int32 [256], replicated, may hold values from 0 to 255, as said below
- pair_list: int32 [1024, 2], P(('blk', 'rep')), may hold values from -1 to 255, as said below
Outputs:
- f_final: float32 [131072], P('blk')
- g_final: float32 [131072], P('blk')
- mapped_x: bfloat16 [131072, 512], P('blk', 'rep')
- mapped_y: bfloat16 [131072, 512], P('blk', 'rep')
Inputs may be any that keep to these rules, and one draw needn't show every extreme that they name: A permutation: block b of either cloud is stored at block position block_owner[b]. `pair_list`: the rows of one index i of blk (those of its devices along rep, in order) begin with 5 to 8 listed pairs and end with rows (-1, -1); some index holds the full 2 * 4 in every draw. A listed pair's first-cloud block has block_owner // 2 = i, its second-cloud block block_owner // 2 = i + d modulo the size of blk, with 1 <= |d| <= 2. No pair is listed twice.
All inputs are finite; a program needn't handle non-finite values.
Results may differ from a plain program's by a relative error of at most 0.0044.
Values may be sent and summed in bfloat16 or wider, within the bound.
A program may use at most 128 MiB of HBM per device.

v0:
```python
import functools
import math

import jax
import jax.numpy as jnp
from jax import lax
from jax.experimental import pallas as pl
from jax.experimental.pallas import tpu as pltpu
from jax.sharding import PartitionSpec as P

D = 512
BLOCK = 512
LANES = 128
GROUPS = BLOCK // LANES
TILES = 9
PAIR_DEV = 4
OFFSETS = (-1, 1, -2, 2)
MIRROR = (1, 0, 3, 2)
PEERS = 9

epsilon = 0.05
K2 = 1.0 / (epsilon * math.log(2.0))
INV_LN2 = 1.0 / math.log(2.0)
NEG = -1.0e30
MESH = pl.DeviceIdType.MESH


def kernel(
    n, pair_ref, owner_ref, x_hbm, y_hbm, m1_ref, m2_ref, f0_ref, g0_ref,
    f_out, g_out, mx_out, my_out,
    own, win, scores, bvec, bias, mpart, spart, lrow, lcol, acc, obuf,
    pot, nrm, lmass, first, ibuf, tile, mbuf,
    load_sem, bsend, brecv, csend, crecv, isend, irecv, psend, precv, osend, orecv,
):
    i = lax.axis_index("blk")
    r = lax.axis_index("rep")
    other = 1 - r

    def chip(offset):
        return lax.rem(i + (n + offset), n)

    def rdma(src, dst, send, recv, where):
        return pltpu.make_async_remote_copy(
            src_ref=src, dst_ref=dst, send_sem=send, recv_sem=recv,
            device_id=where, device_id_type=MESH,
        )

    peers = [(chip(OFFSETS[s]), q) for s in range(4) for q in range(2)] + [(i, other)]

    rows = pl.ds(pl.multiple_of(r * BLOCK, BLOCK), BLOCK)
    load_y = pltpu.make_async_copy(y_hbm.at[rows, :], own.at[0], load_sem.at[0])
    load_x = pltpu.make_async_copy(x_hbm.at[rows, :], own.at[1], load_sem.at[1])
    load_y.start()
    load_x.start()

    barrier = pltpu.get_barrier_semaphore()
    for peer in peers:
        pl.semaphore_signal(barrier, inc=1, device_id=peer, device_id_type=MESH)
    pl.semaphore_wait(barrier, PEERS)

    def step_copy(t, slot):
        ahead = chip(1) if slot % 2 == 0 else chip(-1)
        src = own.at[t] if slot < 2 else win.at[t, slot - 2, r]
        return rdma(src, win.at[t, slot, r], bsend.at[t, slot], brecv.at[t, slot], (ahead, r))

    def cross_copy(t, slot, piece):
        return rdma(
            win.at[t, slot, piece], win.at[t, slot, piece],
            csend.at[t, slot], crecv.at[t, slot], (i, other),
        )

    load_y.wait()
    step_copy(0, 0).start()
    step_copy(0, 1).start()
    load_x.wait()

    pot[0] = g0_ref[r]
    pot[1] = f0_ref[r]
    lmass[0] = jnp.log(m2_ref[r]) * INV_LN2
    lmass[1] = jnp.log(m1_ref[r]) * INV_LN2

    def spread(row, store):
        for l in range(GROUPS):
            store[l : l + 1, :] = row[:, l * LANES : (l + 1) * LANES]

    for t in range(2):
        def square(g, _):
            at = pl.ds(pl.multiple_of(g * 64, 64), 64)
            v = own[t, at, :].astype(jnp.float32)
            v = v * v
            part = v[:, 0:LANES]
            for l in range(1, GROUPS):
                part = part + v[:, l * LANES : (l + 1) * LANES]
            mpart[at, :] = part
            return 0

        lax.fori_loop(0, BLOCK // 64, square, 0)
        total = jnp.sum(jnp.transpose(mpart[...]), axis=0, keepdims=True)
        spread(total * (1.0 / D), lrow)
        nrm[t] = lrow[0:GROUPS, :]
        first[t, 0:GROUPS, :] = K2 * (pot[t] - nrm[t]) + lmass[t]
        first[t, GROUPS : 2 * GROUPS, :] = pot[t]

    line = lax.broadcasted_iota(jnp.int32, (8, LANES), 0)
    listed = jnp.zeros((8, LANES), jnp.float32)
    for p in range(PAIR_DEV):
        a_id = pair_ref[p, 0]
        c_id = pair_ref[p, 1]
        x_at = owner_ref[jnp.maximum(a_id, 0)]
        y_at = owner_ref[jnp.maximum(c_id, 0)]
        offset = lax.rem((y_at >> 1) - i + (n + 2), n) - 2
        slot = jnp.where(offset == -1, 0, jnp.where(offset == 1, 1, jnp.where(offset == -2, 2, 3)))
        at = jnp.where(a_id >= 0, slot * 2 + (y_at & 1), -1)
        amount = ((x_at & 1) + 1).astype(jnp.float32)
        listed = listed + jnp.where(line == at, amount, 0.0)
    first[2] = listed

    def first_copy(k):
        back = MIRROR[k // 2] * 2 + r if k < 8 else 8
        return rdma(first, ibuf.at[back], isend.at[k], irecv.at[back], peers[k])

    def first_wait(k):
        rdma(first, ibuf.at[k], isend.at[k], irecv.at[k], peers[k]).wait_recv()

    for k in range(PEERS):
        first_copy(k).start()
    step_copy(1, 0).start()
    step_copy(1, 1).start()

    def put_scores(side, p, keys):
        dot = lax.dot_general(
            own[1 - side], keys, (((1,), (1,)), ((), ())), preferred_element_type=jnp.float32
        )
        scores[side, p] = dot * (2.0 * K2 / D)

    def home_side(side, _):
        put_scores(side, 0, own[side])
        return 0

    lax.fori_loop(0, 2, home_side, 0)

    def window_scores(side, base):
        def one(j, _):
            put_scores(side, 1 + base * 2 + j, win[side, base + j // 2, j % 2])
            return 0

        lax.fori_loop(0, 4, one, 0)

    def arrive(t, base):
        for slot in (base, base + 1):
            step_copy(t, slot).wait_recv()
            if base == 0:
                step_copy(t, slot + 2).start()
            cross_copy(t, slot, r).start()

    def arrive_cross(t, base):
        for slot in (base, base + 1):
            cross_copy(t, slot, other).wait_recv()

    arrive(0, 0)
    arrive_cross(0, 0)
    window_scores(0, 0)
    arrive(1, 0)
    arrive_cross(1, 0)
    window_scores(1, 0)

    for k in range(PEERS):
        first_wait(k)

    def allow(v, block):
        low = jnp.where(v == 1.0, 0.0, jnp.where(v == 3.0, 0.0, NEG))
        high = jnp.where(v >= 2.0, 0.0, NEG)
        if isinstance(block, int):
            return low if block == 0 else high
        return jnp.where(block == 0, low, high)

    mine = first[2] + ibuf[8, 2]
    bias[0] = allow(mine, r)
    for s in range(4):
        theirs = ibuf[2 * s, 2] + ibuf[2 * s + 1, 2]
        at = MIRROR[s] * 2
        v = jnp.where(r == 0, theirs[at : at + 1, :], theirs[at + 1 : at + 2, :])
        for q in range(2):
            bias[1, 2 * s + q : 2 * s + q + 1, :] = allow(v, q)

    def put_vector(side, home, source):
        for p in range(TILES):
            ref = home if p == 0 else source(p - 1)
            for l in range(GROUPS):
                row = ref[l : l + 1, :]
                if p > 0:
                    row = row + bias[side, p - 1 : p, :]
                at = (p * GROUPS + l) * LANES
                bvec[side, :, at : at + LANES] = jnp.broadcast_to(row, (8, LANES))

    def lse_pass(side):
        def group(g, _):
            at = pl.ds(pl.multiple_of(g * 8, 8), 8)
            terms = []
            for p in range(TILES):
                for l in range(GROUPS):
                    o = (p * GROUPS + l) * LANES
                    terms.append(
                        scores[side, p, at, l * LANES : (l + 1) * LANES]
                        + bvec[side, :, o : o + LANES]
                    )
            highs = [functools.reduce(jnp.maximum, terms[h::4]) for h in range(4)]
            high = jnp.maximum(jnp.maximum(highs[0], highs[1]), jnp.maximum(highs[2], highs[3]))
            sums = [sum(jnp.exp2(t - high) for t in terms[h::4]) for h in range(4)]
            mpart[at, :] = high
            spart[at, :] = (sums[0] + sums[1]) + (sums[2] + sums[3])
            return 0

        lax.fori_loop(0, BLOCK // 8, group, 0)

    def update(side, step):
        t = 1 - side
        turned = jnp.transpose(mpart[...])
        high = jnp.max(turned, axis=0, keepdims=True)
        total = jnp.sum(jnp.transpose(spart[...]) * jnp.exp2(turned - high), axis=0, keepdims=True)
        spread(high + jnp.log(total) * INV_LN2, lrow)
        new = 0.5 * (pot[t] - lrow[0:GROUPS, :] * (1.0 / K2) + nrm[t])
        pot[t] = new
        tile[step, t, 0:GROUPS, :] = K2 * (new - nrm[t]) + lmass[t]
        tile[step, t, GROUPS : 2 * GROUPS, :] = new

    def tile_copy(step, t, k):
        back = MIRROR[k // 2] * 2 + r if k < 8 else 8
        return rdma(
            tile.at[step, t], mbuf.at[step, t, back],
            psend.at[step, t, k], precv.at[step, t, back], peers[k],
        )

    def send_tiles(step, t):
        for k in range(PEERS):
            tile_copy(step, t, k).start()

    def take_tiles(step, t):
        for k in range(PEERS):
            rdma(
                tile.at[step, t], mbuf.at[step, t, k],
                psend.at[step, t, k], precv.at[step, t, k], peers[k],
            ).wait_recv()
        put_vector(t, tile.at[step, t], lambda k: mbuf.at[step, t, k])

    arrive(0, 2)
    arrive_cross(0, 2)
    window_scores(0, 2)
    put_vector(0, first.at[0], lambda k: ibuf.at[k, 0])
    lse_pass(0)
    update(0, 0)
    send_tiles(0, 1)

    arrive(1, 2)
    arrive_cross(1, 2)
    window_scores(1, 2)
    put_vector(1, first.at[1], lambda k: ibuf.at[k, 1])
    lse_pass(1)
    update(1, 0)
    send_tiles(0, 0)

    take_tiles(0, 1)
    lse_pass(1)
    update(1, 1)
    send_tiles(1, 0)

    take_tiles(0, 0)
    lse_pass(0)
    update(0, 1)
    send_tiles(1, 1)

    f_out[r] = pot[1]
    g_out[r] = pot[0]

    def out_copy(side):
        dst = (mx_out, my_out)[side]
        return rdma(obuf.at[side], dst.at[r], osend.at[side], orecv.at[side], (i, other))

    def final(side, out_ref):
        lse_pass(side)

        def column(g, _):
            at = pl.ds(pl.multiple_of(g * 64, 64), 64)
            part = mpart[at, :]
            high = jnp.max(part, axis=1, keepdims=True)
            total = jnp.sum(spart[at, :] * jnp.exp2(part - high), axis=1, keepdims=True)
            lcol[at, :] = jnp.broadcast_to(high + jnp.log(total) * INV_LN2, (64, LANES))
            return 0

        lax.fori_loop(0, BLOCK // 64, column, 0)

        def weigh(p, keys):
            pieces = []
            for l in range(GROUPS):
                o = pl.multiple_of(p * BLOCK + l * LANES, LANES)
                v = scores[side, p, :, l * LANES : (l + 1) * LANES]
                v = v + bvec[side, 0:1, pl.ds(o, LANES)]
                pieces.append(jnp.exp2(v - lcol[...]).astype(jnp.bfloat16))
            return jnp.dot(
                jnp.concatenate(pieces, axis=1), keys, preferred_element_type=jnp.float32
            )

        acc[...] = weigh(0, own[side])

        def one(j, _):
            acc[...] += weigh(j + 1, win[side, j // 2, j % 2])
            return 0

        lax.fori_loop(0, 8, one, 0)
        half = D // 2
        low = acc[:, 0:half].astype(jnp.bfloat16)
        high = acc[:, half:D].astype(jnp.bfloat16)
        obuf[side] = jnp.where(r == 0, high, low)
        out_copy(side).start()
        out_ref[r] = jnp.where(r == 0, low, high)

    take_tiles(1, 0)
    final(0, mx_out)
    take_tiles(1, 1)
    g_out[other] = mbuf[1, 0, 8, GROUPS : 2 * GROUPS, :]
    f_out[other] = mbuf[1, 1, 8, GROUPS : 2 * GROUPS, :]
    final(1, my_out)

    for side in range(2):
        dst = (mx_out, my_out)[side]
        rdma(
            obuf.at[side], dst.at[other], osend.at[side], orecv.at[side], (i, other)
        ).wait_recv()
        out_copy(side).wait_send()
    for t in range(2):
        for slot in range(4):
            step_copy(t, slot).wait_send()
            cross_copy(t, slot, r).wait_send()
    for k in range(PEERS):
        first_copy(k).wait_send()
        for step in range(2):
            for t in range(2):
                tile_copy(step, t, k).wait_send()


def per_device(
    x_points, y_points, first_masses, second_masses, f_start, g_start, block_owner, pair_list
):
    n = lax.axis_size("blk")
    shape = (2, GROUPS, LANES)
    f32, bf16 = jnp.float32, jnp.bfloat16
    dma = pltpu.SemaphoreType.DMA
    smem = pl.BlockSpec(memory_space=pltpu.SMEM)
    vmem = pl.BlockSpec(memory_space=pltpu.VMEM)
    hbm = pl.BlockSpec(memory_space=pl.ANY)
    f, g, mx, my = pl.pallas_call(
        functools.partial(kernel, n),
        out_shape=(
            jax.ShapeDtypeStruct(shape, f32),
            jax.ShapeDtypeStruct(shape, f32),
            jax.ShapeDtypeStruct((2, BLOCK, D // 2), bf16),
            jax.ShapeDtypeStruct((2, BLOCK, D // 2), bf16),
        ),
        in_specs=[smem, smem, hbm, hbm, vmem, vmem, vmem, vmem],
        out_specs=(vmem, vmem, vmem, vmem),
        scratch_shapes=[
            pltpu.VMEM((2, BLOCK, D), bf16),
            pltpu.VMEM((2, 4, 2, BLOCK, D), bf16),
            pltpu.VMEM((2, TILES, BLOCK, BLOCK), f32),
            pltpu.VMEM((2, 8, TILES * BLOCK), f32),
            pltpu.VMEM((2, 8, LANES), f32),
            pltpu.VMEM((BLOCK, LANES), f32),
            pltpu.VMEM((BLOCK, LANES), f32),
            pltpu.VMEM((8, LANES), f32),
            pltpu.VMEM((BLOCK, LANES), f32),
            pltpu.VMEM((BLOCK, D), f32),
            pltpu.VMEM((2, BLOCK, D // 2), bf16),
            pltpu.VMEM(shape, f32),
            pltpu.VMEM(shape, f32),
            pltpu.VMEM(shape, f32),
            pltpu.VMEM((3, 8, LANES), f32),
            pltpu.VMEM((PEERS, 3, 8, LANES), f32),
            pltpu.VMEM((2, 2, 8, LANES), f32),
            pltpu.VMEM((2, 2, PEERS, 8, LANES), f32),
            dma((2,)),
            dma((2, 4)),
            dma((2, 4)),
            dma((2, 4)),
            dma((2, 4)),
            dma((PEERS,)),
            dma((PEERS,)),
            dma((2, 2, PEERS)),
            dma((2, 2, PEERS)),
            dma((2,)),
            dma((2,)),
        ],
        compiler_params=pltpu.CompilerParams(
            collective_id=0, has_side_effects=True, vmem_limit_bytes=60 * 1024 * 1024
        ),
    )(
        pair_list, block_owner, x_points, y_points,
        first_masses.reshape(shape), second_masses.reshape(shape),
        f_start.reshape(shape), g_start.reshape(shape),
    )
    rows = 2 * BLOCK
    return f.reshape(rows), g.reshape(rows), mx.reshape(rows, D // 2), my.reshape(rows, D // 2)


def solution(mesh):
    placed = (
        P("blk", None),
        P("blk", None),
        P("blk"),
        P("blk"),
        P("blk"),
        P("blk"),
        P(),
        P(("blk", "rep"), None),
    )
    return jax.shard_map(
        per_device,
        mesh=mesh,
        in_specs=placed,
        out_specs=(P("blk"), P("blk"), P("blk", "rep"), P("blk", "rep")),
        check_vma=False,
    )
```

profile of v0, /device:TPU:1, one launch (start us, length us, event | category | flops | bytes accessed | tf_op | source)
XLA Modules:
  0.0 112.6 jit_solution(10306286357684757494)
XLA Ops:
  0.6 0.0 copy-start.3
  0.6 0.7 copy-done.3
  1.3 0.7 copy.12.pair_ref
  2.0 106.0 %shard_map.111 = (f32[2,4,128]{2,1,0:T(4,128)}, f32[2,4,128]{2,1,0:T(4,128)}, bf16[2,512,256]{2,1,0:T(8,128)(2,1)}, bf16[2,512,256]{2,1,0:T(8,128)(2,1)}) custom-call(s32[4,2]{1,0:T(4,128)} %copy.12.pair_ref, s32[256]{0:T(256)} %owner_ref.1, bf16[1024,512]{1,0:T(8,128)(2,1)} %x_hbm.1, bf16[1024,512]{1,0:T(8,128)(2,1)} %y_hbm.1, f32[2,4,128]{2,1,0:T(4,128)} %bitcast.10, ...), custom_call_target="tpu_custom_call" | custom-call | tf_op jit(solution)/shard_map/pallas_call | solution.py:351
  107.9 0.0 copy-start.2
  108.0 0.7 copy-done.2
  108.6 0.0 copy-start.1
  108.6 0.6 copy.17
  109.2 0.1 copy-done.1
  109.3 0.6 copy.18
  109.9 0.0 copy-start
  109.9 1.9 %copy.19 = bf16[1024,256]{1,0:T(8,128)(2,1)} copy(bf16[1024,256]{1,0:T(8,128)(2,1)} %bitcast.9) | data formatting | bytes 1048576
  111.8 0.0 copy-done
  111.8 0.8 copy.20
Async XLA Ops:
  0.6 0.7 copy-start.3
  107.9 0.7 copy-start.2
  108.6 0.7 copy-start.1
  109.9 1.9 %copy-start = (bf16[2,512,256]{2,1,0:T(8,128)(2,1)S(1)}, bf16[2,512,256]{2,1,0:T(8,128)(2,1)}, u32[]{:S(2)}) copy-start(bf16[2,512,256]{2,1,0:T(8,128)(2,1)} %get-tuple-element.11) | copy-start | bytes 1572868
where the time goes:
time: 113 us
  Pallas kernels  106 us (94%)
  local copies, waits for them, and re-layouts  6 us (5%)
    pallas_call x1, Pallas kernels, per_device(): pl.pallas_call(functools.partial(kernel, n), out_shape=(jax.ShapeDtypeStr...  106 us
    unnamed x13, local copies, waits for them, and re-layouts  6 us

commit v1 on v0

--- a/solution.py
+++ b/solution.py
@@ -104,8 +104,8 @@
     line = lax.broadcasted_iota(jnp.int32, (8, LANES), 0)
     listed = jnp.zeros((8, LANES), jnp.float32)
     for p in range(PAIR_DEV):
-        a_id = pair_ref[p, 0]
-        c_id = pair_ref[p, 1]
+        a_id = pair_ref[0, p]
+        c_id = pair_ref[1, p]
         x_at = owner_ref[jnp.maximum(a_id, 0)]
         y_at = owner_ref[jnp.maximum(c_id, 0)]
         offset = lax.rem((y_at >> 1) - i + (n + 2), n) - 2
@@ -193,25 +193,32 @@
                 at = (p * GROUPS + l) * LANES
                 bvec[side, :, at : at + LANES] = jnp.broadcast_to(row, (8, LANES))
 
-    def lse_pass(side):
+    def lse_pass(side, tiles=range(TILES), merge=False):
         def group(g, _):
-            at = pl.ds(pl.multiple_of(g * 8, 8), 8)
-            terms = []
-            for p in range(TILES):
-                for l in range(GROUPS):
-                    o = (p * GROUPS + l) * LANES
-                    terms.append(
-                        scores[side, p, at, l * LANES : (l + 1) * LANES]
-                        + bvec[side, :, o : o + LANES]
-                    )
-            highs = [functools.reduce(jnp.maximum, terms[h::4]) for h in range(4)]
-            high = jnp.maximum(jnp.maximum(highs[0], highs[1]), jnp.maximum(highs[2], highs[3]))
-            sums = [sum(jnp.exp2(t - high) for t in terms[h::4]) for h in range(4)]
+            at = pl.ds(pl.multiple_of(g * 32, 32), 32)
+
+            def term(o):
+                b = bvec[side, :, o * LANES : (o + 1) * LANES]
+                p, l = divmod(o, GROUPS)
+                v = scores[side, p, at, l * LANES : (l + 1) * LANES]
+                return v + jnp.concatenate([b] * 4, axis=0)
+
+            spots = [p * GROUPS + l for p in tiles for l in range(GROUPS)]
+            high = jnp.maximum(
+                functools.reduce(jnp.maximum, [term(o) for o in spots[0::2]]),
+                functools.reduce(jnp.maximum, [term(o) for o in spots[1::2]]),
+            )
+            if merge:
+                high = jnp.maximum(high, mpart[at, :])
+            total = sum(jnp.exp2(term(o) - high) for o in spots[0::2])
+            total = total + sum(jnp.exp2(term(o) - high) for o in spots[1::2])
+            if merge:
+                total = total + spart[at, :] * jnp.exp2(mpart[at, :] - high)
             mpart[at, :] = high
-            spart[at, :] = (sums[0] + sums[1]) + (sums[2] + sums[3])
+            spart[at, :] = total
             return 0
 
-        lax.fori_loop(0, BLOCK // 8, group, 0)
+        lax.fori_loop(0, BLOCK // 32, group, 0)
 
     def update(side, step):
         t = 1 - side
@@ -336,6 +343,19 @@
         for step in range(2):
             for t in range(2):
                 tile_copy(step, t, k).wait_send()
+
+
+def emit(*refs):
+    sources, sinks, rooms, (come, go) = refs[0:4], refs[4:8], refs[8:12], refs[12:14]
+    into = [pltpu.make_async_copy(sources[k], rooms[k], come.at[k]) for k in range(4)]
+    out = [pltpu.make_async_copy(rooms[k], sinks[k], go.at[k]) for k in range(4)]
+    for copy in into:
+        copy.start()
+    for k in range(4):
+        into[k].wait()
+        out[k].start()
+    for copy in out:
+        copy.wait()
 
 
 def per_device(
@@ -390,13 +410,21 @@
             dma((2,)),
         ],
         compiler_params=pltpu.CompilerParams(
-            collective_id=0, has_side_effects=True, vmem_limit_bytes=60 * 1024 * 1024
+            collective_id=0, has_side_effects=True, vmem_limit_bytes=63 * 1024 * 1024
         ),
     )(
-        pair_list, block_owner, x_points, y_points,
+        pair_list.T, block_owner, x_points, y_points,
         first_masses.reshape(shape), second_masses.reshape(shape),
         f_start.reshape(shape), g_start.reshape(shape),
     )
+    f, g, mx, my = pl.pallas_call(
+        emit,
+        out_shape=tuple(jax.ShapeDtypeStruct(a.shape, a.dtype) for a in (f, g, mx, my)),
+        in_specs=[hbm] * 4,
+        out_specs=(hbm,) * 4,
+        scratch_shapes=[pltpu.VMEM(a.shape, a.dtype) for a in (f, g, mx, my)] + [dma((4,))] * 2,
+        compiler_params=pltpu.CompilerParams(vmem_limit_bytes=63 * 1024 * 1024),
+    )(f, g, mx, my)
     rows = 2 * BLOCK
     return f.reshape(rows), g.reshape(rows), mx.reshape(rows, D // 2), my.reshape(rows, D // 2)
 

time: 113 us -> 101 us (0.89)
  Pallas kernels: 106 us -> 100 us
  local copies, waits for them, and re-layouts: 6 us -> 0 us
    pallas_call x1, Pallas kernels: 106 us -> 98.3 us  [per_device(): pl.pallas_call(functools.partial(kernel, n), out_shape=(jax.ShapeDtypeStr...]
    unnamed x13 -> x0, local copies, waits for them, and re-layouts: 6 us -> none
    pallas_call x0 -> x1, Pallas kernels: none -> 2.09 us  [per_device(): pl.pallas_call(emit, out_shape=tuple((jax.ShapeDtypeStruct(a.shape, a.dty...]
where the time goes in v1:
time: 101 us
  Pallas kernels  100 us (99%)
    pallas_call x1, Pallas kernels, per_device(): pl.pallas_call(functools.partial(kernel, n), out_shape=(jax.ShapeDtypeStr...  98.3 us
    pallas_call x1, Pallas kernels, per_device(): pl.pallas_call(emit, out_shape=tuple((jax.ShapeDtypeStruct(a.shape, a.dty...  2.09 us

profile of v1, /device:TPU:1, one launch (start us, length us, event | category | flops | bytes accessed | tf_op | source)
XLA Modules:
  0.0 101.0 jit_solution(8967562045551921710)
XLA Ops:
  0.6 98.3 %shard_map.111 = (f32[2,4,128]{2,1,0:T(4,128)}, f32[2,4,128]{2,1,0:T(4,128)}, bf16[2,512,256]{2,1,0:T(8,128)(2,1)}, bf16[2,512,256]{2,1,0:T(8,128)(2,1)}) custom-call(s32[2,4]{1,0:T(2,128)} %bitcast.13, s32[256]{0:T(256)} %owner_ref.1, bf16[1024,512]{1,0:T(8,128)(2,1)} %x_hbm.1, bf16[1024,512]{1,0:T(8,128)(2,1)} %y_hbm.1, f32[2,4,128]{2,1,0:T(4,128)} %bitcast.9, ...), custom_call_target="tpu_custom_call" | custom-call | tf_op jit(solution)/shard_map/pallas_call | solution.py:371
  98.9 2.1 %shard_map.112 = (f32[2,4,128]{2,1,0:T(4,128)}, f32[2,4,128]{2,1,0:T(4,128)}, bf16[2,512,256]{2,1,0:T(8,128)(2,1)}, bf16[2,512,256]{2,1,0:T(8,128)(2,1)}) custom-call(f32[2,4,128]{2,1,0:T(4,128)} %get-tuple-element.12.refs_0_, f32[2,4,128]{2,1,0:T(4,128)} %get-tuple-element.13.refs_1_, bf16[2,512,256]{2,1,0:T(8,128)(2,1)} %get-tuple-element.14.refs_2_, ...), custom_call_target="tpu_custom_call" | custom-call | tf_op jit(solution)/shard_map/pallas_call | solution.py:420

commit v2 on v1

v2 whole, which is shorter than its diff:
```python
import functools
import math

import jax
import jax.numpy as jnp
from jax import lax
from jax.experimental import pallas as pl
from jax.experimental.pallas import tpu as pltpu
from jax.sharding import PartitionSpec as P

D = 512
BLOCK = 512
LANES = 128
GROUPS = BLOCK // LANES
TILES = 9
PAIR_DEV = 4
OFFSETS = (-1, 1, -2, 2)
MIRROR = (1, 0, 3, 2)
PEERS = 9

epsilon = 0.05
K2 = 1.0 / (epsilon * math.log(2.0))
INV_LN2 = 1.0 / math.log(2.0)
NEG = -1.0e30
MESH = pl.DeviceIdType.MESH


def kernel(
    n, pair_ref, owner_ref, x_hbm, y_hbm, m1_ref, m2_ref, f0_ref, g0_ref,
    f_out, g_out, mx_out, my_out,
    own, win, scores, bvec, bias, mpart, spart, lrow, lcol, acol, acc, obuf,
    pot, nrm, lmass, first, ibuf, home_part, part, part_in, tile, tile_in,
    load_sem, bsend, brecv, csend, crecv, isend, irecv, ipair,
    qsend, qrecv, qpair_send, qpair_recv, psend, precv, ppair, osend, orecv,
):
    i = lax.axis_index("blk")
    r = lax.axis_index("rep")
    other = 1 - r
    near = 1 - r

    def chip(offset):
        return lax.rem(i + (n + offset), n)

    ahead = chip(2 * r - 1)

    def rdma(src, dst, send, recv, where):
        return pltpu.make_async_remote_copy(
            src_ref=src, dst_ref=dst, send_sem=send, recv_sem=recv,
            device_id=where, device_id_type=MESH,
        )

    peers = [(chip(o), q) for o in OFFSETS for q in range(2)] + [(i, other)]
    barrier = pltpu.get_barrier_semaphore()
    for peer in peers:
        pl.semaphore_signal(barrier, inc=1, device_id=peer, device_id_type=MESH)
    load_y = pltpu.make_async_copy(y_hbm, own.at[0], load_sem.at[0])
    load_x = pltpu.make_async_copy(x_hbm, own.at[1], load_sem.at[1])
    load_y.start()
    load_x.start()
    pl.semaphore_wait(barrier, PEERS)

    def near_copy(t, c):
        return rdma(
            own.at[t, c], win.at[t, near, c], bsend.at[t, 0, c], brecv.at[t, 0, c], (ahead, r)
        )

    def far_copy(t, c):
        return rdma(
            win.at[t, near, c], win.at[t, 2 + near, c],
            bsend.at[t, 1, c], brecv.at[t, 1, c], (ahead, r),
        )

    def cross_copy(t, far, c, slot):
        at = win.at[t, 2 * far + slot, c]
        return rdma(at, at, csend.at[t, far, c], crecv.at[t, far, c], (i, other))

    def message(src, dst, send, recv, kk, q):
        where = (chip((1 - 2 * r) * (1 + kk)), q)
        return rdma(src, dst.at[r + 2 * kk], send.at[kk, q], recv.at[r + 2 * kk], where)

    load_y.wait()
    near_copy(0, 0).start()
    near_copy(0, 1).start()
    load_x.wait()

    pot[0] = g0_ref[r]
    pot[1] = f0_ref[r]
    lmass[0] = jnp.log(m2_ref[r]) * INV_LN2
    lmass[1] = jnp.log(m1_ref[r]) * INV_LN2

    def spread(row, store):
        for l in range(GROUPS):
            store[l : l + 1, :] = row[:, l * LANES : (l + 1) * LANES]

    for t in range(2):
        def square(g, _):
            at = pl.ds(pl.multiple_of(g * 64, 64), 64)
            v = own[t, r, at, :].astype(jnp.float32)
            v = v * v
            total = v[:, 0:LANES]
            for l in range(1, GROUPS):
                total = total + v[:, l * LANES : (l + 1) * LANES]
            mpart[at, :] = total
            return 0

        lax.fori_loop(0, BLOCK // 64, square, 0)
        total = jnp.sum(jnp.transpose(mpart[...]), axis=0, keepdims=True)
        spread(total * (1.0 / D), lrow)
        nrm[t] = lrow[0:GROUPS, :]

    def vector(t):
        return K2 * (pot[t] - nrm[t]) + lmass[t]

    first[r, 0, 0:GROUPS, :] = vector(0)
    first[r, 0, GROUPS : 2 * GROUPS, :] = pot[0]

    line = lax.broadcasted_iota(jnp.int32, (8, LANES), 0)
    listed = jnp.zeros((8, LANES), jnp.float32)
    for p in range(PAIR_DEV):
        a_id = pair_ref[0, p]
        c_id = pair_ref[1, p]
        x_at = owner_ref[jnp.maximum(a_id, 0)]
        y_at = owner_ref[jnp.maximum(c_id, 0)]
        offset = lax.rem((y_at >> 1) - i + (n + 2), n) - 2
        slot = jnp.where(offset == -1, 0, jnp.where(offset == 1, 1, jnp.where(offset == -2, 2, 3)))
        at = jnp.where(a_id >= 0, slot * 2 + (y_at & 1), -1)
        amount = ((x_at & 1) + 1).astype(jnp.float32)
        listed = listed + jnp.where(line == at, amount, 0.0)
    first[r, 1] = listed

    def first_pair(core):
        return rdma(first.at[core], first.at[core], ipair.at[0], ipair.at[1], (i, other))

    def first_copy(kk, q):
        return message(first, ibuf, isend, irecv, kk, q)

    first_pair(r).start()

    def put_scores(side, p, keys):
        dot = lax.dot_general(
            own[1 - side, r], keys, (((1,), (1,)), ((), ())), preferred_element_type=jnp.float32
        )
        scores[side, p] = dot * (2.0 * K2 / D)

    def home_side(side, _):
        put_scores(side, 0, own[side, r])
        return 0

    lax.fori_loop(0, 2, home_side, 0)

    first_pair(other).wait_recv()
    for kk in range(2):
        for q in range(2):
            first_copy(kk, q).start()

    def allow(v, block):
        low = jnp.where(v == 1.0, 0.0, jnp.where(v == 3.0, 0.0, NEG))
        high = jnp.where(v >= 2.0, 0.0, NEG)
        if isinstance(block, int):
            return low if block == 0 else high
        return jnp.where(block == 0, low, high)

    bias[0] = allow(first[0, 1] + first[1, 1], r)

    def window_scores(side, slot):
        def one(c, _):
            put_scores(side, 1 + slot * 2 + c, win[side, slot, c])
            return 0

        lax.fori_loop(0, 2, one, 0)

    def turn_vector():
        v = vector(1)
        row = jnp.concatenate([v[l : l + 1, :] for l in range(GROUPS)], axis=1)
        acol[...] = jnp.transpose(jnp.broadcast_to(row, (LANES, BLOCK)))

    def column_part(p, store, extra):
        for l in range(GROUPS):
            lanes = slice(l * LANES, (l + 1) * LANES)

            def term(k):
                at = slice(k * 64, (k + 1) * 64)
                return scores[0, p, at, lanes] + acol[at, :]

            high = functools.reduce(jnp.maximum, [term(k) for k in range(8)])
            total = sum(jnp.exp2(term(k) - high) for k in range(8))
            top = jnp.max(high, axis=0, keepdims=True)
            total = jnp.sum(total * jnp.exp2(high - top), axis=0, keepdims=True)
            store[l : l + 1, :] = top if extra is None else top + extra
            store[GROUPS + l : GROUPS + l + 1, :] = total

    def window_parts(step, low, high):
        def one(j, _):
            column_part(j + 1, part.at[step, j // 2, j % 2, r], bias[0, pl.ds(j, 1), :])
            return 0

        lax.fori_loop(low, high, one, 0)

    def part_give(step, kk):
        for c in range(2):
            at = part.at[step, r + 2 * kk, c, r]
            rdma(
                at, at, qpair_send.at[step, kk, c], qpair_recv.at[step, kk, c], (i, other)
            ).start()

    def part_copy(step, kk, c):
        slot = 1 - r + 2 * kk
        return rdma(
            part.at[step, slot, c], part_in.at[step, r + 2 * kk],
            qsend.at[step, kk, c], qrecv.at[step, r + 2 * kk], (chip((1 - 2 * r) * (1 + kk)), c),
        )

    def part_got(step, kk, c):
        at = part.at[step, 1 - r + 2 * kk, c, other]
        return rdma(
            at, at, qpair_send.at[step, kk, c], qpair_recv.at[step, kk, c], (i, other)
        )

    def part_send(step, kk):
        for c in range(2):
            part_got(step, kk, c).wait_recv()
            part_copy(step, kk, c).start()

    def put_vector(side, home, source):
        for p in range(TILES):
            ref = home if p == 0 else source((p - 1) // 2, (p - 1) % 2)
            for l in range(GROUPS):
                row = ref[l : l + 1, :]
                if p > 0:
                    row = row + bias[side, p - 1 : p, :]
                at = (p * GROUPS + l) * LANES
                bvec[side, :, at : at + LANES] = jnp.broadcast_to(row, (8, LANES))

    def lse_pass(side, tiles=range(TILES), merge=False):
        def group(g, _):
            at = pl.ds(pl.multiple_of(g * 32, 32), 32)

            def term(o):
                b = bvec[side, :, o * LANES : (o + 1) * LANES]
                p, l = divmod(o, GROUPS)
                v = scores[side, p, at, l * LANES : (l + 1) * LANES]
                return v + jnp.concatenate([b] * 4, axis=0)

            spots = [p * GROUPS + l for p in tiles for l in range(GROUPS)]
            high = jnp.maximum(
                functools.reduce(jnp.maximum, [term(o) for o in spots[0::2]]),
                functools.reduce(jnp.maximum, [term(o) for o in spots[1::2]]),
            )
            if merge:
                high = jnp.maximum(high, mpart[at, :])
            total = sum(jnp.exp2(term(o) - high) for o in spots[0::2])
            total = total + sum(jnp.exp2(term(o) - high) for o in spots[1::2])
            if merge:
                total = total + spart[at, :] * jnp.exp2(mpart[at, :] - high)
            mpart[at, :] = high
            spart[at, :] = total
            return 0

        lax.fori_loop(0, BLOCK // 32, group, 0)

    def row_update():
        turned = jnp.transpose(mpart[...])
        high = jnp.max(turned, axis=0, keepdims=True)
        total = jnp.sum(jnp.transpose(spart[...]) * jnp.exp2(turned - high), axis=0, keepdims=True)
        spread(high + jnp.log(total) * INV_LN2, lrow)
        move(1, lrow[0:GROUPS, :])

    def move(t, lse):
        pot[t] = 0.5 * (pot[t] - lse * (1.0 / K2) + nrm[t])

    def column_update(step):
        for s in range(4):
            part_copy_wait(step, s)
        tops = [home_part[step, 0:GROUPS, :]]
        totals = [home_part[step, GROUPS : 2 * GROUPS, :]]
        for s in range(4):
            for a in range(2):
                tops.append(part_in[step, s, a, 0:GROUPS, :])
                totals.append(part_in[step, s, a, GROUPS : 2 * GROUPS, :])
        top = functools.reduce(jnp.maximum, tops)
        total = sum(v * jnp.exp2(h - top) for h, v in zip(tops, totals))
        move(0, top + jnp.log(total) * INV_LN2)

    def part_copy_wait(step, s):
        rdma(
            part_in.at[step, s], part_in.at[step, s], qsend.at[step, 0, 0],
            qrecv.at[step, s], (i, other),
        ).wait_recv()

    def tile_pair(m, core):
        at = tile.at[m, core]
        return rdma(at, at, ppair.at[m, 0], ppair.at[m, 1], (i, other))

    def tile_copy(m, kk, q):
        return message(tile.at[m], tile_in.at[m], psend.at[m], precv.at[m], kk, q)

    def send_tile(m, t):
        tile[m, r, 0:GROUPS, :] = vector(t)
        tile[m, r, GROUPS : 2 * GROUPS, :] = pot[t]
        tile_pair(m, r).start()

    def relay_tile(m):
        tile_pair(m, other).wait_recv()
        for kk in range(2):
            for q in range(2):
                tile_copy(m, kk, q).start()

    def take_tile(m, side):
        for s in range(4):
            at = tile_in.at[m, s]
            rdma(at, at, psend.at[m, 0, 0], precv.at[m, s], (i, other)).wait_recv()
        put_vector(side, tile.at[m, r], lambda s, q: tile_in.at[m, s, q])

    def first_take():
        for s in range(4):
            at = ibuf.at[s]
            rdma(at, at, isend.at[0, 0], irecv.at[s], (i, other)).wait_recv()
        for s in range(4):
            theirs = ibuf[s, 0, 1] + ibuf[s, 1, 1]
            at = MIRROR[s] * 2
            v = jnp.where(r == 0, theirs[at : at + 1, :], theirs[at + 1 : at + 2, :])
            for q in range(2):
                bias[1, 2 * s + q : 2 * s + q + 1, :] = allow(v, q)
        put_vector(0, first.at[r, 0], lambda s, q: ibuf.at[s, q, 0])

    def near_arrive(t, c):
        near_copy(t, c).wait_recv()
        far_copy(t, c).start()
        cross_copy(t, 0, c, near).start()

    def far_arrive(t, c):
        far_copy(t, c).wait_recv()
        cross_copy(t, 1, c, near).start()

    def crossed(t, far):
        for c in range(2):
            cross_copy(t, far, c, other_near).wait_recv()

    other_near = r

    turn_vector()
    column_part(0, home_part.at[0], None)
    near_arrive(0, 0)
    near_arrive(0, 1)
    near_copy(1, 0).start()
    near_copy(1, 1).start()
    window_scores(0, near)
    crossed(0, 0)
    window_scores(0, other_near)
    window_parts(0, 0, 4)
    part_give(0, 0)
    first_take()
    lse_pass(0, range(0, 5))
    part_send(0, 0)

    far_arrive(0, 0)
    far_arrive(0, 1)
    window_scores(0, 2 + near)
    crossed(0, 1)
    window_scores(0, 2 + other_near)
    window_parts(0, 4, 8)
    part_give(0, 1)
    lse_pass(0, range(5, 9), True)
    part_send(0, 1)
    row_update()
    turn_vector()
    column_part(0, home_part.at[1], None)
    window_parts(1, 0, 8)
    for kk in range(2):
        part_give(1, kk)
    near_arrive(1, 0)
    for kk in range(2):
        part_send(1, kk)

    column_update(0)
    send_tile(0, 0)
    relay_tile(0)
    near_arrive(1, 1)
    column_update(1)
    send_tile(1, 0)
    relay_tile(1)
    window_scores(1, near)
    crossed(1, 0)
    window_scores(1, other_near)

    take_tile(0, 0)
    lse_pass(0)
    row_update()
    send_tile(2, 1)
    f_out[r] = pot[1]
    g_out[r] = pot[0]
    g_out[other] = tile[1, other, GROUPS : 2 * GROUPS, :]
    relay_tile(2)
    f_out[other] = tile[2, other, GROUPS : 2 * GROUPS, :]
    take_tile(1, 0)

    def out_copy(side):
        dst = (mx_out, my_out)[side]
        return rdma(obuf.at[side], dst.at[r], osend.at[side], orecv.at[side], (i, other))

    def final(side, out_ref):
        lse_pass(side)

        def column(g, _):
            at = pl.ds(pl.multiple_of(g * 64, 64), 64)
            part = mpart[at, :]
            high = jnp.max(part, axis=1, keepdims=True)
            total = jnp.sum(spart[at, :] * jnp.exp2(part - high), axis=1, keepdims=True)
            lcol[at, :] = jnp.broadcast_to(high + jnp.log(total) * INV_LN2, (64, LANES))
            return 0

        lax.fori_loop(0, BLOCK // 64, column, 0)

        def weigh(p, keys):
            pieces = []
            for l in range(GROUPS):
                o = pl.multiple_of(p * BLOCK + l * LANES, LANES)
                v = scores[side, p, :, l * LANES : (l + 1) * LANES]
                v = v + bvec[side, 0:1, pl.ds(o, LANES)]
                pieces.append(jnp.exp2(v - lcol[...]).astype(jnp.bfloat16))
            return jnp.dot(
                jnp.concatenate(pieces, axis=1), keys, preferred_element_type=jnp.float32
            )

        acc[...] = weigh(0, own[side, r])

        def one(j, _):
            acc[...] += weigh(j + 1, win[side, j // 2, j % 2])
            return 0

        lax.fori_loop(0, 8, one, 0)
        half = D // 2
        low = acc[:, 0:half].astype(jnp.bfloat16)
        high = acc[:, half:D].astype(jnp.bfloat16)
        obuf[side] = jnp.where(r == 0, high, low)
        out_copy(side).start()
        out_ref[r] = jnp.where(r == 0, low, high)

    final(0, mx_out)
    far_arrive(1, 0)
    far_arrive(1, 1)
    window_scores(1, 2 + near)
    crossed(1, 1)
    window_scores(1, 2 + other_near)
    take_tile(2, 1)
    final(1, my_out)

    for side in range(2):
        dst = (mx_out, my_out)[side]
        rdma(
            obuf.at[side], dst.at[other], osend.at[side], orecv.at[side], (i, other)
        ).wait_recv()
        out_copy(side).wait_send()
    for t in range(2):
        for c in range(2):
            near_copy(t, c).wait_send()
            far_copy(t, c).wait_send()
            for far in range(2):
                cross_copy(t, far, c, near).wait_send()
    first_pair(r).wait_send()
    for m in range(3):
        tile_pair(m, r).wait_send()
    for kk in range(2):
        for q in range(2):
            first_copy(kk, q).wait_send()
            for m in range(3):
                tile_copy(m, kk, q).wait_send()
            for step in range(2):
                part_copy(step, kk, q).wait_send()
                at = part.at[step, r + 2 * kk, q, r]
                rdma(
                    at, at, qpair_send.at[step, kk, q], qpair_recv.at[step, kk, q], (i, other)
                ).wait_send()


def emit(*refs):
    sources, sinks, rooms, (come, go) = refs[0:4], refs[4:8], refs[8:12], refs[12:14]
    into = [pltpu.make_async_copy(sources[k], rooms[k], come.at[k]) for k in range(4)]
    out = [pltpu.make_async_copy(rooms[k], sinks[k], go.at[k]) for k in range(4)]
    for copy in into:
        copy.start()
    for k in range(4):
        into[k].wait()
        out[k].start()
    for copy in out:
        copy.wait()


def per_device(
    x_points, y_points, first_masses, second_masses, f_start, g_start, block_owner, pair_list
):
    n = lax.axis_size("blk")
    shape = (2, GROUPS, LANES)
    f32, bf16 = jnp.float32, jnp.bfloat16
    dma = pltpu.SemaphoreType.DMA
    smem = pl.BlockSpec(memory_space=pltpu.SMEM)
    vmem = pl.BlockSpec(memory_space=pltpu.VMEM)
    hbm = pl.BlockSpec(memory_space=pl.ANY)
    f, g, mx, my = pl.pallas_call(
        functools.partial(kernel, n),
        out_shape=(
            jax.ShapeDtypeStruct(shape, f32),
            jax.ShapeDtypeStruct(shape, f32),
            jax.ShapeDtypeStruct((2, BLOCK, D // 2), bf16),
            jax.ShapeDtypeStruct((2, BLOCK, D // 2), bf16),
        ),
        in_specs=[smem, smem, hbm, hbm, vmem, vmem, vmem, vmem],
        out_specs=(vmem, vmem, vmem, vmem),
        scratch_shapes=[
            pltpu.VMEM((2, 2, BLOCK, D), bf16),
            pltpu.VMEM((2, 4, 2, BLOCK, D), bf16),
            pltpu.VMEM((2, TILES, BLOCK, BLOCK), f32),
            pltpu.VMEM((2, 8, TILES * BLOCK), f32),
            pltpu.VMEM((2, 8, LANES), f32),
            pltpu.VMEM((BLOCK, LANES), f32),
            pltpu.VMEM((BLOCK, LANES), f32),
            pltpu.VMEM((8, LANES), f32),
            pltpu.VMEM((BLOCK, LANES), f32),
            pltpu.VMEM((BLOCK, LANES), f32),
            pltpu.VMEM((BLOCK, D), f32),
            pltpu.VMEM((2, BLOCK, D // 2), bf16),
            pltpu.VMEM(shape, f32),
            pltpu.VMEM(shape, f32),
            pltpu.VMEM(shape, f32),
            pltpu.VMEM((2, 2, 8, LANES), f32),
            pltpu.VMEM((4, 2, 2, 8, LANES), f32),
            pltpu.VMEM((2, 8, LANES), f32),
            pltpu.VMEM((2, 4, 2, 2, 8, LANES), f32),
            pltpu.VMEM((2, 4, 2, 8, LANES), f32),
            pltpu.VMEM((3, 2, 8, LANES), f32),
            pltpu.VMEM((3, 4, 2, 8, LANES), f32),
            dma((2,)),
            dma((2, 2, 2)),
            dma((2, 2, 2)),
            dma((2, 2, 2)),
            dma((2, 2, 2)),
            dma((2, 2)),
            dma((4,)),
            dma((2,)),
            dma((2, 2, 2)),
            dma((2, 4)),
            dma((2, 2, 2)),
            dma((2, 2, 2)),
            dma((3, 2, 2)),
            dma((3, 4)),
            dma((3, 2)),
            dma((2,)),
            dma((2,)),
        ],
        compiler_params=pltpu.CompilerParams(
            collective_id=0, has_side_effects=True, vmem_limit_bytes=63 * 1024 * 1024
        ),
    )(
        pair_list.T, block_owner, x_points.reshape(2, BLOCK, D), y_points.reshape(2, BLOCK, D),
        first_masses.reshape(shape), second_masses.reshape(shape),
        f_start.reshape(shape), g_start.reshape(shape),
    )
    f, g, mx, my = pl.pallas_call(
        emit,
        out_shape=tuple(jax.ShapeDtypeStruct(a.shape, a.dtype) for a in (f, g, mx, my)),
        in_specs=[hbm] * 4,
        out_specs=(hbm,) * 4,
        scratch_shapes=[pltpu.VMEM(a.shape, a.dtype) for a in (f, g, mx, my)] + [dma((4,))] * 2,
        compiler_params=pltpu.CompilerParams(vmem_limit_bytes=63 * 1024 * 1024),
    )(f, g, mx, my)
    rows = 2 * BLOCK
    return f.reshape(rows), g.reshape(rows), mx.reshape(rows, D // 2), my.reshape(rows, D // 2)


def solution(mesh):
    placed = (
        P("blk", None),
        P("blk", None),
        P("blk"),
        P("blk"),
        P("blk"),
        P("blk"),
        P(),
        P(("blk", "rep"), None),
    )
    return jax.shard_map(
        per_device,
        mesh=mesh,
        in_specs=placed,
        out_specs=(P("blk"), P("blk"), P("blk", "rep"), P("blk", "rep")),
        check_vma=False,
    )
```

time: 101 us -> 88.9 us (0.88)
  Pallas kernels: 100 us -> 88.1 us
    pallas_call x1, Pallas kernels: 98.3 us -> 86 us  [per_device(): pl.pallas_call(functools.partial(kernel, n), out_shape=(jax.ShapeDtypeStr...]
where the time goes in v2:
time: 88.9 us; the launch traced here: 88.7 us
  Pallas kernels  88.1 us (99%)
    pallas_call x1, Pallas kernels, per_device(): pl.pallas_call(functools.partial(kernel, n), out_shape=(jax.ShapeDtypeStr...  86 us
    pallas_call x1, Pallas kernels, per_device(): pl.pallas_call(emit, out_shape=tuple((jax.ShapeDtypeStruct(a.shape, a.dty...  2.09 us

profile of v2, /device:TPU:1, one launch (start us, length us, event | category | flops | bytes accessed | tf_op | source)
XLA Modules:
  0.0 88.7 jit_solution(2808321814166546331)
XLA Ops:
  0.6 86.0 %shard_map.111 = (f32[2,4,128]{2,1,0:T(4,128)}, f32[2,4,128]{2,1,0:T(4,128)}, bf16[2,512,256]{2,1,0:T(8,128)(2,1)}, bf16[2,512,256]{2,1,0:T(8,128)(2,1)}) custom-call(s32[2,4]{1,0:T(2,128)} %bitcast.17, s32[256]{0:T(256)} %owner_ref.1, bf16[2,512,512]{2,1,0:T(8,128)(2,1)} %bitcast.11, bf16[2,512,512]{2,1,0:T(8,128)(2,1)} %bitcast.12, f32[2,4,128]{2,1,0:T(4,128)} %bitcast.13, ...), custom_call_target="tpu_custom_call" | custom-call | tf_op jit(solution)/shard_map/pallas_call | solution.py:499
  86.6 2.1 %shard_map.112 = (f32[2,4,128]{2,1,0:T(4,128)}, f32[2,4,128]{2,1,0:T(4,128)}, bf16[2,512,256]{2,1,0:T(8,128)(2,1)}, bf16[2,512,256]{2,1,0:T(8,128)(2,1)}) custom-call(f32[2,4,128]{2,1,0:T(4,128)} %get-tuple-element.12.refs_0_, f32[2,4,128]{2,1,0:T(4,128)} %get-tuple-element.13.refs_1_, bf16[2,512,256]{2,1,0:T(8,128)(2,1)} %get-tuple-element.14.refs_2_, ...), custom_call_target="tpu_custom_call" | custom-call | tf_op jit(solution)/shard_map/pallas_call | solution.py:558

commit v3 on v2

--- a/solution.py
+++ b/solution.py
@@ -26,12 +26,12 @@
 
 
 def kernel(
-    n, pair_ref, owner_ref, x_hbm, y_hbm, m1_ref, m2_ref, f0_ref, g0_ref,
+    n, pair_ref, owner_ref, x_hbm, y_hbm, m1_hbm, m2_hbm, f0_hbm, g0_hbm,
     f_out, g_out, mx_out, my_out,
     own, win, scores, bvec, bias, mpart, spart, lrow, lcol, acol, acc, obuf,
-    pot, nrm, lmass, first, ibuf, home_part, part, part_in, tile, tile_in,
+    kept, ended, begin, pot, nrm, lmass, first, ibuf, home_part, part, part_in, tile, tile_in,
     load_sem, bsend, brecv, csend, crecv, isend, irecv, ipair,
-    qsend, qrecv, qpair_send, qpair_recv, psend, precv, ppair, osend, orecv,
+    qsend, qrecv, qpair_send, qpair_recv, psend, precv, ppair, osend, orecv, kept_sem,
 ):
     i = lax.axis_index("blk")
     r = lax.axis_index("rep")
@@ -53,10 +53,15 @@
     barrier = pltpu.get_barrier_semaphore()
     for peer in peers:
         pl.semaphore_signal(barrier, inc=1, device_id=peer, device_id_type=MESH)
-    load_y = pltpu.make_async_copy(y_hbm, own.at[0], load_sem.at[0])
-    load_x = pltpu.make_async_copy(x_hbm, own.at[1], load_sem.at[1])
-    load_y.start()
-    load_x.start()
+    loads = [
+        pltpu.make_async_copy((y_hbm, x_hbm)[t].at[c], own.at[t, c], load_sem.at[2 * t + c])
+        for t in range(2)
+        for c in range(2)
+    ]
+    for k, source in enumerate((g0_hbm, f0_hbm, m2_hbm, m1_hbm)):
+        loads.append(pltpu.make_async_copy(source, begin.at[k], load_sem.at[4 + k]))
+    for load in loads:
+        load.start()
     pl.semaphore_wait(barrier, PEERS)
 
     def near_copy(t, c):
@@ -78,15 +83,15 @@
         where = (chip((1 - 2 * r) * (1 + kk)), q)
         return rdma(src, dst.at[r + 2 * kk], send.at[kk, q], recv.at[r + 2 * kk], where)
 
-    load_y.wait()
-    near_copy(0, 0).start()
-    near_copy(0, 1).start()
-    load_x.wait()
-
-    pot[0] = g0_ref[r]
-    pot[1] = f0_ref[r]
-    lmass[0] = jnp.log(m2_ref[r]) * INV_LN2
-    lmass[1] = jnp.log(m1_ref[r]) * INV_LN2
+    for c in range(2):
+        loads[c].wait()
+        near_copy(0, c).start()
+    for load in loads[2:]:
+        load.wait()
+
+    for t in range(2):
+        pot[t] = begin[t, r]
+        lmass[t] = jnp.log(begin[2 + t, r]) * INV_LN2
 
     def spread(row, store):
         for l in range(GROUPS):
@@ -169,6 +174,13 @@
 
         lax.fori_loop(0, 2, one, 0)
 
+    def one_score(side, slot, c):
+        def one(_, carry):
+            put_scores(side, 1 + slot * 2 + c, win[side, slot, c])
+            return carry
+
+        one(0, 0)
+
     def turn_vector():
         v = vector(1)
         row = jnp.concatenate([v[l : l + 1, :] for l in range(GROUPS)], axis=1)
@@ -189,15 +201,16 @@
             store[l : l + 1, :] = top if extra is None else top + extra
             store[GROUPS + l : GROUPS + l + 1, :] = total
 
-    def window_parts(step, low, high):
-        def one(j, _):
+    def window_parts(step, low, high, stride=1):
+        def one(k, _):
+            j = low + k * stride
             column_part(j + 1, part.at[step, j // 2, j % 2, r], bias[0, pl.ds(j, 1), :])
             return 0
 
-        lax.fori_loop(low, high, one, 0)
-
-    def part_give(step, kk):
-        for c in range(2):
+        lax.fori_loop(0, (high - low + stride - 1) // stride, one, 0)
+
+    def part_give(step, kk, blocks=(0, 1)):
+        for c in blocks:
             at = part.at[step, r + 2 * kk, c, r]
             rdma(
                 at, at, qpair_send.at[step, kk, c], qpair_recv.at[step, kk, c], (i, other)
@@ -233,13 +246,13 @@
 
     def lse_pass(side, tiles=range(TILES), merge=False):
         def group(g, _):
-            at = pl.ds(pl.multiple_of(g * 32, 32), 32)
+            at = pl.ds(pl.multiple_of(g * 64, 64), 64)
 
             def term(o):
                 b = bvec[side, :, o * LANES : (o + 1) * LANES]
                 p, l = divmod(o, GROUPS)
                 v = scores[side, p, at, l * LANES : (l + 1) * LANES]
-                return v + jnp.concatenate([b] * 4, axis=0)
+                return v + jnp.concatenate([b] * 8, axis=0)
 
             spots = [p * GROUPS + l for p in tiles for l in range(GROUPS)]
             high = jnp.maximum(
@@ -256,7 +269,7 @@
             spart[at, :] = total
             return 0
 
-        lax.fori_loop(0, BLOCK // 32, group, 0)
+        lax.fori_loop(0, BLOCK // 64, group, 0)
 
     def row_update():
         turned = jnp.transpose(mpart[...])
@@ -332,11 +345,19 @@
         far_copy(t, c).wait_recv()
         cross_copy(t, 1, c, near).start()
 
-    def crossed(t, far):
-        for c in range(2):
+    def crossed(t, far, blocks=(0, 1)):
+        for c in blocks:
             cross_copy(t, far, c, other_near).wait_recv()
 
     other_near = r
+
+    def ended_copy(t):
+        return pltpu.make_async_copy(ended.at[t], (g_out, f_out)[t], kept_sem.at[2 + t])
+
+    def kept_copy(side):
+        return pltpu.make_async_copy(
+            kept.at[side], (mx_out, my_out)[side].at[r], kept_sem.at[side]
+        )
 
     turn_vector()
     column_part(0, home_part.at[0], None)
@@ -354,14 +375,19 @@
     part_send(0, 0)
 
     far_arrive(0, 0)
+    one_score(0, 2 + near, 0)
+    crossed(0, 1, (0,))
+    one_score(0, 2 + other_near, 0)
+    window_parts(0, 4, 8, 2)
+    part_give(0, 1, (0,))
     far_arrive(0, 1)
-    window_scores(0, 2 + near)
-    crossed(0, 1)
-    window_scores(0, 2 + other_near)
-    window_parts(0, 4, 8)
-    part_give(0, 1)
+    one_score(0, 2 + near, 1)
+    crossed(0, 1, (1,))
+    one_score(0, 2 + other_near, 1)
+    window_parts(0, 5, 8, 2)
+    part_give(0, 1, (1,))
+    part_send(0, 1)
     lse_pass(0, range(5, 9), True)
-    part_send(0, 1)
     row_update()
     turn_vector()
     column_part(0, home_part.at[1], None)
@@ -387,18 +413,18 @@
     lse_pass(0)
     row_update()
     send_tile(2, 1)
-    f_out[r] = pot[1]
-    g_out[r] = pot[0]
-    g_out[other] = tile[1, other, GROUPS : 2 * GROUPS, :]
     relay_tile(2)
-    f_out[other] = tile[2, other, GROUPS : 2 * GROUPS, :]
+    for t in range(2):
+        ended[t, r] = pot[t]
+        ended[t, other] = tile[1 + t, other, GROUPS : 2 * GROUPS, :]
+        ended_copy(t).start()
     take_tile(1, 0)
 
     def out_copy(side):
         dst = (mx_out, my_out)[side]
         return rdma(obuf.at[side], dst.at[r], osend.at[side], orecv.at[side], (i, other))
 
-    def final(side, out_ref):
+    def final(side):
         lse_pass(side)
 
         def column(g, _):
@@ -411,39 +437,38 @@
 
         lax.fori_loop(0, BLOCK // 64, column, 0)
 
-        def weigh(p, keys):
+        def weigh(first_tile, count, keys):
             pieces = []
-            for l in range(GROUPS):
-                o = pl.multiple_of(p * BLOCK + l * LANES, LANES)
-                v = scores[side, p, :, l * LANES : (l + 1) * LANES]
-                v = v + bvec[side, 0:1, pl.ds(o, LANES)]
-                pieces.append(jnp.exp2(v - lcol[...]).astype(jnp.bfloat16))
+            for k in range(count):
+                p = first_tile + k
+                for l in range(GROUPS):
+                    o = pl.multiple_of(p * BLOCK + l * LANES, LANES)
+                    v = scores[side, p, :, l * LANES : (l + 1) * LANES]
+                    v = v + bvec[side, 0:1, pl.ds(o, LANES)]
+                    pieces.append(jnp.exp2(v - lcol[...]).astype(jnp.bfloat16))
             return jnp.dot(
                 jnp.concatenate(pieces, axis=1), keys, preferred_element_type=jnp.float32
             )
 
-        acc[...] = weigh(0, own[side, r])
-
-        def one(j, _):
-            acc[...] += weigh(j + 1, win[side, j // 2, j % 2])
-            return 0
-
-        lax.fori_loop(0, 8, one, 0)
+        acc[...] = weigh(0, 1, own[side, r])
+
+        acc[...] += weigh(1, 8, win[side].reshape(8 * BLOCK, D))
         half = D // 2
         low = acc[:, 0:half].astype(jnp.bfloat16)
         high = acc[:, half:D].astype(jnp.bfloat16)
         obuf[side] = jnp.where(r == 0, high, low)
         out_copy(side).start()
-        out_ref[r] = jnp.where(r == 0, low, high)
-
-    final(0, mx_out)
-    far_arrive(1, 0)
-    far_arrive(1, 1)
+        kept[side] = jnp.where(r == 0, low, high)
+        kept_copy(side).start()
+
+    final(0)
+    for c in range(2):
+        far_arrive(1, c)
     window_scores(1, 2 + near)
     crossed(1, 1)
     window_scores(1, 2 + other_near)
     take_tile(2, 1)
-    final(1, my_out)
+    final(1)
 
     for side in range(2):
         dst = (mx_out, my_out)[side]
@@ -451,6 +476,8 @@
             obuf.at[side], dst.at[other], osend.at[side], orecv.at[side], (i, other)
         ).wait_recv()
         out_copy(side).wait_send()
+        kept_copy(side).wait()
+        ended_copy(side).wait()
     for t in range(2):
         for c in range(2):
             near_copy(t, c).wait_send()
@@ -494,7 +521,6 @@
     f32, bf16 = jnp.float32, jnp.bfloat16
     dma = pltpu.SemaphoreType.DMA
     smem = pl.BlockSpec(memory_space=pltpu.SMEM)
-    vmem = pl.BlockSpec(memory_space=pltpu.VMEM)
     hbm = pl.BlockSpec(memory_space=pl.ANY)
     f, g, mx, my = pl.pallas_call(
         functools.partial(kernel, n),
@@ -504,8 +530,8 @@
             jax.ShapeDtypeStruct((2, BLOCK, D // 2), bf16),
             jax.ShapeDtypeStruct((2, BLOCK, D // 2), bf16),
         ),
-        in_specs=[smem, smem, hbm, hbm, vmem, vmem, vmem, vmem],
-        out_specs=(vmem, vmem, vmem, vmem),
+        in_specs=[smem, smem] + [hbm] * 6,
+        out_specs=(hbm,) * 4,
         scratch_shapes=[
             pltpu.VMEM((2, 2, BLOCK, D), bf16),
             pltpu.VMEM((2, 4, 2, BLOCK, D), bf16),
@@ -519,6 +545,9 @@
             pltpu.VMEM((BLOCK, LANES), f32),
             pltpu.VMEM((BLOCK, D), f32),
             pltpu.VMEM((2, BLOCK, D // 2), bf16),
+            pltpu.VMEM((2, BLOCK, D // 2), bf16),
+            pltpu.VMEM((2,) + shape, f32),
+            pltpu.VMEM((4,) + shape, f32),
             pltpu.VMEM(shape, f32),
             pltpu.VMEM(shape, f32),
             pltpu.VMEM(shape, f32),
@@ -529,7 +558,7 @@
             pltpu.VMEM((2, 4, 2, 8, LANES), f32),
             pltpu.VMEM((3, 2, 8, LANES), f32),
             pltpu.VMEM((3, 4, 2, 8, LANES), f32),
-            dma((2,)),
+            dma((8,)),
             dma((2, 2, 2)),
             dma((2, 2, 2)),
             dma((2, 2, 2)),
@@ -546,6 +575,7 @@
             dma((3, 2)),
             dma((2,)),
             dma((2,)),
+            dma((4,)),
         ],
         compiler_params=pltpu.CompilerParams(
             collective_id=0, has_side_effects=True, vmem_limit_bytes=63 * 1024 * 1024

time: 88.9 us -> 84.7 us (0.953)
  Pallas kernels: 88.1 us -> 83.8 us
    pallas_call x1, Pallas kernels: 86 us -> 81.7 us  [per_device(): pl.pallas_call(functools.partial(kernel, n), out_shape=(jax.ShapeDtypeStr...]
where the time goes in v3:
time: 84.7 us; the launch traced here: 84.6 us
  Pallas kernels  83.8 us (99%)
    pallas_call x1, Pallas kernels, per_device(): pl.pallas_call(functools.partial(kernel, n), out_shape=(jax.ShapeDtypeStr...  81.7 us
    pallas_call x1, Pallas kernels, per_device(): pl.pallas_call(emit, out_shape=tuple((jax.ShapeDtypeStruct(a.shape, a.dty...  2.09 us

profile of v3, /device:TPU:1, one launch (start us, length us, event | category | flops | bytes accessed | tf_op | source)
XLA Modules:
  0.0 84.6 jit_solution(9477170254851366153)
XLA Ops:
  0.6 81.7 %shard_map.111 = (f32[2,4,128]{2,1,0:T(4,128)}, f32[2,4,128]{2,1,0:T(4,128)}, bf16[2,512,256]{2,1,0:T(8,128)(2,1)}, bf16[2,512,256]{2,1,0:T(8,128)(2,1)}) custom-call(s32[2,4]{1,0:T(2,128)} %bitcast.17, s32[256]{0:T(256)} %owner_ref.1, bf16[2,512,512]{2,1,0:T(8,128)(2,1)} %bitcast.11, bf16[2,512,512]{2,1,0:T(8,128)(2,1)} %bitcast.12, f32[2,4,128]{2,1,0:T(4,128)} %bitcast.13, ...), custom_call_target="tpu_custom_call" | custom-call | tf_op jit(solution)/shard_map/pallas_call | solution.py:525
  82.3 2.1 %shard_map.112 = (f32[2,4,128]{2,1,0:T(4,128)}, f32[2,4,128]{2,1,0:T(4,128)}, bf16[2,512,256]{2,1,0:T(8,128)(2,1)}, bf16[2,512,256]{2,1,0:T(8,128)(2,1)}) custom-call(f32[2,4,128]{2,1,0:T(4,128)} %get-tuple-element.12.refs_0_, f32[2,4,128]{2,1,0:T(4,128)} %get-tuple-element.13.refs_1_, bf16[2,512,256]{2,1,0:T(8,128)(2,1)} %get-tuple-element.14.refs_2_, ...), custom_call_target="tpu_custom_call" | custom-call | tf_op jit(solution)/shard_map/pallas_call | solution.py:588

commit v4 on v3

--- a/solution.py
+++ b/solution.py
@@ -28,7 +28,7 @@
 def kernel(
     n, pair_ref, owner_ref, x_hbm, y_hbm, m1_hbm, m2_hbm, f0_hbm, g0_hbm,
     f_out, g_out, mx_out, my_out,
-    own, win, scores, bvec, bias, mpart, spart, lrow, lcol, acol, acc, obuf,
+    own, win, scores, bvec, bias, mpart, spart, lrow, lcol, acol, obuf,
     kept, ended, begin, pot, nrm, lmass, first, ibuf, home_part, part, part_in, tile, tile_in,
     load_sem, bsend, brecv, csend, crecv, isend, irecv, ipair,
     qsend, qrecv, qpair_send, qpair_recv, psend, precv, ppair, osend, orecv, kept_sem,
@@ -390,13 +390,14 @@
     lse_pass(0, range(5, 9), True)
     row_update()
     turn_vector()
+    window_parts(1, 4, 8)
+    part_give(1, 1)
+    window_parts(1, 0, 4)
+    part_give(1, 0)
+    part_send(1, 1)
+    near_arrive(1, 0)
+    part_send(1, 0)
     column_part(0, home_part.at[1], None)
-    window_parts(1, 0, 8)
-    for kk in range(2):
-        part_give(1, kk)
-    near_arrive(1, 0)
-    for kk in range(2):
-        part_send(1, kk)
 
     column_update(0)
     send_tile(0, 0)
@@ -413,12 +414,12 @@
     lse_pass(0)
     row_update()
     send_tile(2, 1)
+    take_tile(1, 0)
     relay_tile(2)
     for t in range(2):
         ended[t, r] = pot[t]
         ended[t, other] = tile[1 + t, other, GROUPS : 2 * GROUPS, :]
         ended_copy(t).start()
-    take_tile(1, 0)
 
     def out_copy(side):
         dst = (mx_out, my_out)[side]
@@ -450,12 +451,10 @@
                 jnp.concatenate(pieces, axis=1), keys, preferred_element_type=jnp.float32
             )
 
-        acc[...] = weigh(0, 1, own[side, r])
-
-        acc[...] += weigh(1, 8, win[side].reshape(8 * BLOCK, D))
+        total = weigh(0, 1, own[side, r]) + weigh(1, 8, win[side].reshape(8 * BLOCK, D))
         half = D // 2
-        low = acc[:, 0:half].astype(jnp.bfloat16)
-        high = acc[:, half:D].astype(jnp.bfloat16)
+        low = total[:, 0:half].astype(jnp.bfloat16)
+        high = total[:, half:D].astype(jnp.bfloat16)
         obuf[side] = jnp.where(r == 0, high, low)
         out_copy(side).start()
         kept[side] = jnp.where(r == 0, low, high)
@@ -543,7 +542,6 @@
             pltpu.VMEM((8, LANES), f32),
             pltpu.VMEM((BLOCK, LANES), f32),
             pltpu.VMEM((BLOCK, LANES), f32),
-            pltpu.VMEM((BLOCK, D), f32),
             pltpu.VMEM((2, BLOCK, D // 2), bf16),
             pltpu.VMEM((2, BLOCK, D // 2), bf16),
             pltpu.VMEM((2,) + shape, f32),

time: 84.7 us -> 84 us (level)
  Pallas kernels: 83.8 us -> 82.4 us
    pallas_call x1, Pallas kernels: 81.7 us -> 80.3 us  [per_device(): pl.pallas_call(functools.partial(kernel, n), out_shape=(jax.ShapeDtypeStr...]
where the time goes in v4:
time: 84 us; the launch traced here: 83.2 us
  Pallas kernels  82.4 us (98%)
    pallas_call x1, Pallas kernels, per_device(): pl.pallas_call(functools.partial(kernel, n), out_shape=(jax.ShapeDtypeStr...  80.3 us
    pallas_call x1, Pallas kernels, per_device(): pl.pallas_call(emit, out_shape=tuple((jax.ShapeDtypeStruct(a.shape, a.dty...  2.09 us

profile of v4, /device:TPU:1, one launch (start us, length us, event | category | flops | bytes accessed | tf_op | source)
XLA Modules:
  0.0 83.2 jit_solution(583723319626702836)
XLA Ops:
  0.6 80.3 %shard_map.111 = (f32[2,4,128]{2,1,0:T(4,128)}, f32[2,4,128]{2,1,0:T(4,128)}, bf16[2,512,256]{2,1,0:T(8,128)(2,1)}, bf16[2,512,256]{2,1,0:T(8,128)(2,1)}) custom-call(s32[2,4]{1,0:T(2,128)} %bitcast.17, s32[256]{0:T(256)} %owner_ref.1, bf16[2,512,512]{2,1,0:T(8,128)(2,1)} %bitcast.11, bf16[2,512,512]{2,1,0:T(8,128)(2,1)} %bitcast.12, f32[2,4,128]{2,1,0:T(4,128)} %bitcast.13, ...), custom_call_target="tpu_custom_call" | custom-call | tf_op jit(solution)/shard_map/pallas_call | solution.py:524
  80.9 2.1 %shard_map.112 = (f32[2,4,128]{2,1,0:T(4,128)}, f32[2,4,128]{2,1,0:T(4,128)}, bf16[2,512,256]{2,1,0:T(8,128)(2,1)}, bf16[2,512,256]{2,1,0:T(8,128)(2,1)}) custom-call(f32[2,4,128]{2,1,0:T(4,128)} %get-tuple-element.12.refs_0_, f32[2,4,128]{2,1,0:T(4,128)} %get-tuple-element.13.refs_1_, bf16[2,512,256]{2,1,0:T(8,128)(2,1)} %get-tuple-element.14.refs_2_, ...), custom_call_target="tpu_custom_call" | custom-call | tf_op jit(solution)/shard_map/pallas_call | solution.py:586

commit v5 on v4

--- a/solution.py
+++ b/solution.py
@@ -246,13 +246,13 @@
 
     def lse_pass(side, tiles=range(TILES), merge=False):
         def group(g, _):
-            at = pl.ds(pl.multiple_of(g * 64, 64), 64)
+            at = pl.ds(pl.multiple_of(g * 128, 128), 128)
 
             def term(o):
                 b = bvec[side, :, o * LANES : (o + 1) * LANES]
                 p, l = divmod(o, GROUPS)
                 v = scores[side, p, at, l * LANES : (l + 1) * LANES]
-                return v + jnp.concatenate([b] * 8, axis=0)
+                return v + jnp.concatenate([b] * 16, axis=0)
 
             spots = [p * GROUPS + l for p in tiles for l in range(GROUPS)]
             high = jnp.maximum(
@@ -269,7 +269,7 @@
             spart[at, :] = total
             return 0
 
-        lax.fori_loop(0, BLOCK // 64, group, 0)
+        lax.fori_loop(0, BLOCK // 128, group, 0)
 
     def row_update():
         turned = jnp.transpose(mpart[...])

time: 84 us -> 84 us (level)
  no operation moved by 1% of the time
where the time goes in v5:
time: 84 us; the launch traced here: 83.1 us
  Pallas kernels  82.3 us (98%)
    pallas_call x1, Pallas kernels, per_device(): pl.pallas_call(functools.partial(kernel, n), out_shape=(jax.ShapeDtypeStr...  80.2 us
    pallas_call x1, Pallas kernels, per_device(): pl.pallas_call(emit, out_shape=tuple((jax.ShapeDtypeStruct(a.shape, a.dty...  2.09 us

profile of v5, /device:TPU:1, one launch (start us, length us, event | category | flops | bytes accessed | tf_op | source)
XLA Modules:
  0.0 83.1 jit_solution(7591339334226962886)
XLA Ops:
  0.6 80.2 %shard_map.111 = (f32[2,4,128]{2,1,0:T(4,128)}, f32[2,4,128]{2,1,0:T(4,128)}, bf16[2,512,256]{2,1,0:T(8,128)(2,1)}, bf16[2,512,256]{2,1,0:T(8,128)(2,1)}) custom-call(s32[2,4]{1,0:T(2,128)} %bitcast.17, s32[256]{0:T(256)} %owner_ref.1, bf16[2,512,512]{2,1,0:T(8,128)(2,1)} %bitcast.11, bf16[2,512,512]{2,1,0:T(8,128)(2,1)} %bitcast.12, f32[2,4,128]{2,1,0:T(4,128)} %bitcast.13, ...), custom_call_target="tpu_custom_call" | custom-call | tf_op jit(solution)/shard_map/pallas_call | solution.py:524
  80.9 2.1 %shard_map.112 = (f32[2,4,128]{2,1,0:T(4,128)}, f32[2,4,128]{2,1,0:T(4,128)}, bf16[2,512,256]{2,1,0:T(8,128)(2,1)}, bf16[2,512,256]{2,1,0:T(8,128)(2,1)}) custom-call(f32[2,4,128]{2,1,0:T(4,128)} %get-tuple-element.12.refs_0_, f32[2,4,128]{2,1,0:T(4,128)} %get-tuple-element.13.refs_1_, bf16[2,512,256]{2,1,0:T(8,128)(2,1)} %get-tuple-element.14.refs_2_, ...), custom_call_target="tpu_custom_call" | custom-call | tf_op jit(solution)/shard_map/pallas_call | solution.py:586
